TPU v7x, 32 devices: a whole 2x2x4 slice. The times are simulated.
32 devices in a mesh: sp: 2 (over core), py: 4 (over z), pz: 4 (over y, x).
Axes of the slice: x: 2, y: 2, z: 4, core: 2. Of those that a mesh axis runs over, the one named last changes fastest.
Arguments:
- concentration: float32 [8, 128, 128, 128], P('sp', 'py', 'pz'), may hold values from -1 to 1.1
- mobility: float32 [8, 8], replicated, may hold values from 0.1 to 0.6
- kappa: float32 [8], replicated, may hold values from 0.5 to 2
- well_depth: float32 [8], P('sp'), may hold values from 0.5 to 2
Outputs:
- updated: float32 [8, 128, 128, 128], P('sp', 'py', 'pz')
All inputs are finite; a program needn't handle non-finite values.
Results may differ from a plain program's by a relative error of at most 0.000084.
Values sent between devices are 32-bit elements; how exact they have to be, the bound alone decides.
A program may use at most 128 MiB of HBM per device.

v0:
```python
import math
import jax
import jax.numpy as jnp
from jax import lax
from jax.sharding import PartitionSpec as P


def tables(count):
    modes = jnp.arange(count, dtype=jnp.int32)
    product = modes[:, None] * modes[None, :] % count
    angle = 2.0 * math.pi * product.astype(jnp.float32) / count
    return (jnp.cos(angle), jnp.sin(angle))


def wave_square(index, count):
    freq = jnp.where(index < count // 2, index, index - count).astype(jnp.float32)
    return (2.0 * math.pi * freq / count) ** 2


def contract(form, values, table):
    return jnp.einsum(form, values, table, precision=lax.Precision.HIGHEST)


def rotate(spectrum, form, count, forward):
    cosine, sine = tables(count)
    real_part, imag_part = (spectrum[0], spectrum[1])
    real_cos = contract(form, real_part, cosine)
    real_sin = contract(form, real_part, sine)
    imag_cos = contract(form, imag_part, cosine)
    imag_sin = contract(form, imag_part, sine)
    if forward:
        return jnp.stack([real_cos + imag_sin, imag_cos - real_sin])
    return jnp.stack([real_cos - imag_sin, imag_cos + real_sin])


def per_device(concentration, mobility, kappa, well_depth):
    local_species, rows_x, rows_y, depth = concentration.shape
    count_sp = lax.axis_size("sp")
    count_py = lax.axis_size("py")
    count_pz = lax.axis_size("pz")
    full_x = rows_x * count_py
    full_y = rows_y * count_pz
    half_depth = depth // 2
    bulk = well_depth[:, None, None, None] * (
        concentration * concentration * concentration - concentration
    )
    fields = jnp.stack([concentration, bulk])
    cosine, sine = tables(depth)
    alternate = (1 - 2 * (jnp.arange(depth, dtype=jnp.int32) % 2)).astype(jnp.float32)
    spectrum = jnp.stack(
        [
            contract("fsxyz,zk->fsxyk", fields, cosine[:, :half_depth]),
            -contract("fsxyz,zk->fsxyk", fields, sine[:, :half_depth]),
        ]
    )
    spectrum = lax.all_to_all(spectrum, "pz", split_axis=5, concat_axis=4, tiled=True)
    own_lines = spectrum.shape[5]
    highest = contract("fsxyz,z->fsxy", fields, alternate)
    highest = lax.all_gather(highest, "pz", axis=3, tiled=True)
    highest = jnp.stack([highest, jnp.zeros_like(highest)])[..., None]
    spectrum = jnp.concatenate([spectrum, highest], axis=5)
    z_modes = jnp.concatenate(
        [
            lax.axis_index("pz") * own_lines + jnp.arange(own_lines, dtype=jnp.int32),
            jnp.full((1,), half_depth, jnp.int32),
        ]
    )
    spectrum = rotate(spectrum, "fsxyz,yk->fsxkz", full_y, True)
    spectrum = lax.all_to_all(
        lax.all_to_all(spectrum, "sp", split_axis=4, concat_axis=2, tiled=True),
        "py",
        split_axis=4,
        concat_axis=3,
        tiled=True,
    )
    spectrum = rotate(spectrum, "fsxyz,xk->fskyz", full_x, True)
    narrow = spectrum.shape[4]
    lines = spectrum.shape[5]
    y_start = (lax.axis_index("sp") * count_py + lax.axis_index("py")) * narrow
    ksq_x = wave_square(jnp.arange(full_x, dtype=jnp.int32), full_x)
    ksq_y = wave_square(y_start + jnp.arange(narrow, dtype=jnp.int32), full_y)
    ksq_z = wave_square(z_modes, depth)
    ksq = ksq_x[:, None, None] + ksq_y[None, :, None] + ksq_z[None, None, :]
    c_hat = spectrum[:, 0]
    drive = spectrum[:, 1] + kappa[None, :, None, None, None] * ksq[None, None] * c_hat
    mix = jnp.einsum("ij,rjxyz->rixyz", mobility, drive, precision=lax.Precision.HIGHEST)
    stiff = 0.5 * (jnp.diagonal(mobility) * kappa)[:, None, None, None] * (ksq * ksq)[None]
    new_hat = (c_hat * (1.0 + stiff)[None] - 0.5 * ksq[None, None] * mix) / (1.0 + stiff)[None]
    new_hat = rotate(new_hat, "sxyz,xk->skyz", full_x, False)
    moved = lax.all_to_all(
        lax.all_to_all(new_hat, "sp", split_axis=1, concat_axis=3, tiled=True),
        "py",
        split_axis=2,
        concat_axis=3,
        tiled=True,
    )
    moved = moved.reshape(2, local_species, rows_x, count_py, count_sp, narrow, lines)
    moved = moved.transpose(0, 1, 2, 4, 3, 5, 6).reshape(2, local_species, rows_x, full_y, lines)
    moved = rotate(moved, "sxyz,yk->sxkz", full_y, False)
    main = moved[..., : lines - 1]
    highest = moved[0, :, :, :, lines - 1]
    main = lax.all_to_all(main, "pz", split_axis=3, concat_axis=4, tiled=True)
    highest = lax.dynamic_slice_in_dim(highest, lax.axis_index("pz") * rows_y, rows_y, 2)
    weight = jnp.where(jnp.arange(half_depth, dtype=jnp.int32) == 0, 1.0, 2.0).astype(jnp.float32)
    result = contract("sxyk,kz->sxyz", main[0] * weight, cosine[:half_depth]) - contract(
        "sxyk,kz->sxyz", main[1] * weight, sine[:half_depth]
    )
    result = result + highest[..., None] * alternate[None, None, None, :]
    return result * (1.0 / (full_x * full_y * depth))


def solution(mesh):
    in_specs = (P("sp", "py", "pz", None), P(), P(), P("sp"))
    out_specs = P("sp", "py", "pz", None)
    return jax.shard_map(
        per_device, mesh=mesh, in_specs=in_specs, out_specs=out_specs, check_vma=False
    )
```

profile of v0, /device:TPU:0, one launch (start us, length us, event | category | flops | bytes accessed | tf_op | source)
XLA Modules:
  0.0 783.9 jit_solution(356317510580128092)
XLA Ops:
  13.9 16.6 %copy.169 = f32[2,2,4,32,32,64]{4,3,2,1,0,5:T(8,128)} copy(f32[2,2,4,32,32,64]{5,4,3,2,1,0:T(8,128)} %pad_maximum_fusion) | data formatting | bytes 8388608 | tf_op jit(solution)/shard_map/stack | solution.py:50
  30.5 11.5 %reshape.175 = f32[4,1,262144]{2,1,0:T(1,128)} reshape(f32[64,2,2,4,32,32]{5,4,3,2,1,0:T(8,128)} %bitcast.208) | data formatting | bytes 8388608
  47.2 17.9 %fusion.9 = f32[1,2,4,32,32]{4,0,3,2,1:T(1,128)S(1)} fusion(f32[1,4,32,32,128]{4,3,2,1,0:T(8,128)} %copy-done.3, f32[1,4,32,32,128]{4,3,2,1,0:T(8,128)S(1)} %bitcast.224), kind=kOutput, calls=%fused_computation.25 | convolution fusion | flops 13632640 | bytes 4227072 | tf_op jit(solution)/shard_map/fsxyz,z->fsxy/dot_general | solution.py:21
  65.2 36.4 %all_gather.3 = f32[2,4,32,128]{2,1,0,3:T(4,128)S(1)} all-gather(f32[2,4,32,32]{2,1,0,3:T(4,128)S(1)} %bitcast.230), channel_id=1, replica_groups=mesh['sp'=2,'py'=4,'pz'=4] {'pz'}, dimensions={3}, use_global_device_ids=true | all-gather | bytes 163840 | tf_op jit(solution)/shard_map/all_gather | solution.py:59
  102.4 16.1 %reduce = f32[4,262144]{1,0:T(4,128)} reduce(f32[4,1,262144]{2,1,0:T(1,128)} %all-to-all-done, f32[]{:T(128)} %broadcast.307), dimensions={1}, to_apply=%all_to_all.72.reduce_sub_computation | reduce | bytes 8388612 | tf_op jit(solution)/shard_map/all_to_all | solution.py:56
  118.5 13.7 %reshape.176 = f32[64,2,2,4,32,32]{5,4,3,2,1,0:T(8,128)} reshape(f32[4,262144]{1,0:T(4,128)} %reduce) | data formatting | bytes 8388608
  132.2 21.0 %copy.171 = f32[2,2,4,32,4,32,16]{5,4,3,6,2,1,0:T(4,128)} copy(f32[2,2,4,32,4,32,16]{5,3,2,1,0,6,4:T(8,128)} %bitcast.209) | data formatting | bytes 8388608 | tf_op jit(solution)/shard_map/all_to_all | solution.py:56
  153.2 13.6 %all_to_all.75 = f32[2,2,4,32,128,16]{4,3,5,2,1,0:T(8,128)} reshape(f32[2,2,4,32,4,32,16]{5,4,3,6,2,1,0:T(4,128)} %copy.171) | data formatting | bytes 8388608 | tf_op jit(solution)/shard_map/all_to_all | solution.py:56
  180.4 15.2 %copy.177 = f32[2,2,4,32,128,17]{3,2,5,1,0,4:T(4,128)} copy(f32[2,2,4,32,128,17]{4,3,5,2,1,0:T(8,128)} %pad_maximum_fusion.1) | data formatting | bytes 8912896 | tf_op jit(solution)/shard_map/stack | solution.py:32
  195.6 22.2 %reshape.177 = f32[2,1,557056]{2,1,0:T(1,128)} reshape(f32[128,2,2,17,4,32]{5,4,3,2,1,0:T(4,128)} %bitcast.204) | data formatting | bytes 8912896
  217.8 12.4 %all_to_all.99 = f32[2,1,557056]{2,1,0:T(1,128)} all-to-all(f32[2,1,557056]{2,1,0:T(1,128)} %reshape.177), channel_id=1, replica_groups=mesh['sp'=2,'py'=4,'pz'=4] {'sp'}, dimensions={0} | all-to-all | bytes 8912896 | tf_op jit(solution)/shard_map/all_to_all | solution.py:70
  230.2 17.5 %reduce.1 = f32[2,557056]{1,0:T(2,128)} reduce(f32[2,1,557056]{2,1,0:T(1,128)} %all_to_all.99, f32[]{:T(128)} %broadcast.307), dimensions={1}, to_apply=%all_to_all.76.reduce_sub_computation | reduce | bytes 8912900 | tf_op jit(solution)/shard_map/all_to_all | solution.py:70
  247.7 23.0 %reshape.178 = f32[128,2,2,17,4,32]{5,4,3,2,1,0:T(4,128)} reshape(f32[2,557056]{1,0:T(2,128)} %reduce.1) | data formatting | bytes 8912896
  270.7 20.5 %copy.258 = f32[2,2,4,32,2,64,17]{5,4,3,6,2,1,0:T(2,128)} copy(f32[2,2,4,32,2,64,17]{3,2,6,1,0,5,4:T(4,128)} %bitcast.205) | data formatting | bytes 8912896 | tf_op jit(solution)/shard_map/all_to_all | solution.py:70
  299.5 17.6 %copy.180 = f32[2,2,8,32,64,17]{3,2,5,1,0,4:T(8,128)} copy(f32[2,2,8,32,64,17]{4,3,5,2,1,0:T(8,128)} %bitcast.216) | data formatting | bytes 8912896 | tf_op jit(solution)/shard_map/all_to_all | solution.py:70
  317.0 21.0 %reshape.179 = f32[4,1,278528]{2,1,0:T(1,128)} reshape(f32[64,2,2,17,8,32]{5,4,3,2,1,0:T(8,128)} %bitcast.206) | data formatting | bytes 8912896
  346.1 96.4 %all-to-all-done.2 = f32[4,1,278528]{2,1,0:T(1,128)} async-done(((f32[4,1,278528]{2,1,0:T(1,128)}), f32[4,1,278528]{2,1,0:T(1,128)}, u32[]{:S(2)}, u32[]{:S(2)}) %all-to-all-start.2) | async-done | bytes 4456480 | tf_op jit(solution)/shard_map/all_to_all | solution.py:69
  442.5 16.0 %reduce.2 = f32[4,278528]{1,0:T(4,128)} reduce(f32[4,1,278528]{2,1,0:T(1,128)} %all-to-all-done.2, f32[]{:T(128)} %broadcast.307), dimensions={1}, to_apply=%all_to_all.80.reduce_sub_computation | reduce | bytes 8912900 | tf_op jit(solution)/shard_map/all_to_all | solution.py:69
  458.5 14.6 %reshape.180 = f32[64,2,2,17,8,32]{5,4,3,2,1,0:T(8,128)} reshape(f32[4,278528]{1,0:T(4,128)} %reduce.2) | data formatting | bytes 8912896
  490.5 10.5 %copy.273 = f32[1,2,8,4,32,16,17]{4,3,6,5,2,1,0:T(4,128)} copy(f32[1,2,8,4,32,16,17]{4,5,3,6,2,1,0:T(8,128)} %get-tuple-element.5) | data formatting | bytes 4456448 | tf_op jit(solution)/shard_map/squeeze | solution.py:26
  576.2 55.0 %all_to_all.101 = f32[4,1,139264]{2,1,0:T(1,128)} all-to-all(f32[4,1,139264]{2,1,0:T(1,128)S(1)} %reshape.181), channel_id=1, replica_groups=mesh['sp'=2,'py'=4,'pz'=4] {'py'}, dimensions={0} | all-to-all | bytes 4456448 | tf_op jit(solution)/shard_map/all_to_all | solution.py:90
  647.3 12.1 %copy.204 = f32[2,4,32,4,32,17]{2,4,5,3,1,0:T(8,128)} copy(f32[2,4,32,4,32,17]{4,1,5,0,2,3:T(4,128)} %bitcast.218) | data formatting | bytes 4456448 | tf_op jit(solution)/shard_map/all_to_all | solution.py:90
  713.9 24.5 %all-to-all-done.5 = f32[4,1,131072]{2,1,0:T(1,128)} async-done(((f32[4,1,131072]{2,1,0:T(1,128)}), f32[4,1,131072]{2,1,0:T(1,128)}, u32[]{:S(2)}, u32[]{:S(2)}) %all-to-all-start.5) | async-done | bytes 2097184 | tf_op jit(solution)/shard_map/all_to_all | solution.py:102
  752.2 11.8 %copy.216 = f32[2,4,32,4,32,16]{4,5,3,2,1,0:T(8,128)} copy(f32[2,4,32,4,32,16]{2,5,1,0,4,3:T(8,128)} %bitcast.220) | data formatting | bytes 4194304 | tf_op jit(solution)/shard_map/all_to_all | solution.py:102
  (99 shorter events, 246.0 us)
Async XLA Ops:
  0.0 343.1 %copy-start = (f32[8,8]{1,0:T(8,128)S(1)}, f32[8,8]{1,0:T(8,128)}, u32[]{:S(2)}) copy-start(f32[8,8]{1,0:T(8,128)} %param.5) | copy-start | bytes 772
  0.0 2.7 copy-start.2
  0.3 2.5 copy-start.8
  0.5 5.6 copy-start.10
  2.7 3.5 copy-start.3
  42.0 59.9 %all-to-all-start = ((f32[4,1,262144]{2,1,0:T(1,128)}), f32[4,1,262144]{2,1,0:T(1,128)}, u32[]{:S(2)}, u32[]{:S(2)}) async-start(f32[4,1,262144]{2,1,0:T(1,128)} %reshape.175), calls=%async_computation | async-start | bytes 8388608 | tf_op jit(solution)/shard_map/all_to_all | solution.py:56
  166.9 3.9 copy-start.1
  338.0 5.9 copy-start.12
  338.0 104.5 %all-to-all-start.2 = ((f32[4,1,278528]{2,1,0:T(1,128)}), f32[4,1,278528]{2,1,0:T(1,128)}, u32[]{:S(2)}, u32[]{:S(2)}) async-start(f32[4,1,278528]{2,1,0:T(1,128)} %reshape.179), calls=%async_computation.2 | async-start | bytes 8912896 | tf_op jit(solution)/shard_map/all_to_all | solution.py:69
  532.4 5.0 copy-start.4
  532.4 5.0 copy-start.5
  540.5 3.1 copy-start.7
  544.1 3.6 copy-start.6
  709.3 29.1 %all-to-all-start.5 = ((f32[4,1,131072]{2,1,0:T(1,128)}), f32[4,1,131072]{2,1,0:T(1,128)}, u32[]{:S(2)}, u32[]{:S(2)}) async-start(f32[4,1,131072]{2,1,0:T(1,128)} %reshape.183), calls=%async_computation.5 | async-start | bytes 4194304 | tf_op jit(solution)/shard_map/all_to_all | solution.py:102
  764.0 4.4 copy-start.11
  768.3 6.8 copy-start.9
where the time goes:
time: 795 us; the launch traced here: 784 us
  local copies, waits for them, and re-layouts  354 us (45%)
  waiting for transfers between devices  121 us (15%)
  blocking collectives  109 us (14%)
  matrix products  105 us (13%)
  other arithmetic  78.8 us (10%)
  starting transfers between devices  14.7 us (2%)
    unnamed x36, local copies, waits for them, and re-layouts  135 us
    dot_general x21, matrix products, contract(): return jnp.einsum(form, values, table, precision=lax.Precision.HIGHEST)  102 us
    all_to_all x1, waiting for transfers between devices, per_device(): lax.all_to_all(lax.all_to_all(spectrum, 'sp', split_axis=4, concat_axis=2...  96.4 us
    all_to_all x1, blocking collectives, per_device(): lax.all_to_all(lax.all_to_all(new_hat, 'sp', split_axis=1, concat_axis=3,...  55 us
    all_to_all x3, local copies, waits for them, and re-layouts, per_device(): lax.all_to_all(spectrum, 'sp', split_axis=4, concat_axis=2, tiled=True)  46.4 us
    squeeze x4, local copies, waits for them, and re-layouts, rotate(): real_part, imag_part = (spectrum[0], spectrum[1])  37.2 us
    all_gather x1, blocking collectives, per_device(): highest = lax.all_gather(highest, 'pz', axis=3, tiled=True)  36.4 us
    all_to_all x3, local copies, waits for them, and re-layouts, per_device(): lax.all_to_all(spectrum, 'pz', split_axis=5, concat_axis=4, tiled=True)  35.2 us
  transfers between devices with their start and end apart: 3, of which 2 were waited for; matrix products, arithmetic and copies ran while one was open for 3% of the time, Pallas kernels for 0%

commit v1 on v0

--- a/solution.py
+++ b/solution.py
@@ -66,13 +66,20 @@
         ]
     )
     spectrum = rotate(spectrum, "fsxyz,yk->fsxkz", full_y, True)
-    spectrum = lax.all_to_all(
-        lax.all_to_all(spectrum, "sp", split_axis=4, concat_axis=2, tiled=True),
-        "py",
-        split_axis=4,
-        concat_axis=3,
-        tiled=True,
-    )
+    x = lax.all_to_all(spectrum, "sp", split_axis=4, concat_axis=2, tiled=True)
+    ways, here = (lax.axis_size("py"), lax.axis_index("py"))
+    width = x.shape[4] // ways
+    dims = list(x.shape)
+    dims[4] = width
+    height = dims[3]
+    dims[3] = height * ways
+    full = jnp.zeros(dims, x.dtype)
+    for mask in range(ways):
+        part = lax.dynamic_slice_in_dim(x, (here ^ mask) * width, width, axis=4)
+        if mask:
+            part = lax.ppermute(part, "py", [(d, d ^ mask) for d in range(ways)])
+        full = lax.dynamic_update_slice_in_dim(full, part, (here ^ mask) * height, axis=3)
+    spectrum = full
     spectrum = rotate(spectrum, "fsxyz,xk->fskyz", full_x, True)
     narrow = spectrum.shape[4]
     lines = spectrum.shape[5]

time: 795 us -> 1060 us (1.33)
  local copies, waits for them, and re-layouts: 354 us -> 568 us
  waiting for transfers between devices: 121 us -> 187 us
  other arithmetic: 78.8 us -> 62 us
    dynamic_update_slice x0 -> x4, local copies, waits for them, and re-layouts: none -> 283 us  [per_device(): lax.dynamic_update_slice_in_dim(full, part, (here ^ mask) * height, axis=3)]
    ppermute x0 -> x3, waiting for transfers between devices: none -> 163 us  [per_device(): part = lax.ppermute(part, 'py', [(d, d ^ mask) for d in range(ways)])]
    all_to_all x1 -> x0, waiting for transfers between devices: 96.4 us -> none  [per_device(): lax.all_to_all(lax.all_to_all(spectrum, 'sp', split_axis=4, concat_axis=2...]
    all_to_all x4 -> x1, local copies, waits for them, and re-layouts: 56.3 us -> 16 us  [per_device(): x = lax.all_to_all(spectrum, 'sp', split_axis=4, concat_axis=2, tiled=True)]
    squeeze x4 -> x0, local copies, waits for them, and re-layouts: 37.2 us -> none  [rotate(): real_part, imag_part = (spectrum[0], spectrum[1])]
    unnamed x36 -> x30, local copies, waits for them, and re-layouts: 135 us -> 99.7 us
    dynamic_slice x0 -> x4, local copies, waits for them, and re-layouts: none -> 27 us  [per_device(): part = lax.dynamic_slice_in_dim(x, (here ^ mask) * width, width, axis=4)]
    ppermute x0 -> x3, local copies, waits for them, and re-layouts: none -> 20.8 us  [per_device(): part = lax.ppermute(part, 'py', [(d, d ^ mask) for d in range(ways)])]
  transfers between devices with their start and end apart: 3 -> 5, of which waited for: 2 -> 3; matrix products, arithmetic and copies ran while one was open for 3% -> 23% of each run, Pallas kernels for 0% -> 0%
where the time goes in v1:
time: 1060 us; the launch traced here: 1050 us
  local copies, waits for them, and re-layouts  568 us (54%)
  waiting for transfers between devices  187 us (18%)
  blocking collectives  110 us (10%)
  matrix products  104 us (10%)
  other arithmetic  62 us (6%)
  starting transfers between devices  14 us (1%)
    dynamic_update_slice x4, local copies, waits for them, and re-layouts, per_device(): lax.dynamic_update_slice_in_dim(full, part, (here ^ mask) * height, axis=3)  283 us
    ppermute x3, waiting for transfers between devices, per_device(): part = lax.ppermute(part, 'py', [(d, d ^ mask) for d in range(ways)])  163 us
    dot_general x21, matrix products, contract(): return jnp.einsum(form, values, table, precision=lax.Precision.HIGHEST)  100 us
    unnamed x30, local copies, waits for them, and re-layouts  99.7 us
    all_to_all x1, blocking collectives, per_device(): lax.all_to_all(lax.all_to_all(new_hat, 'sp', split_axis=1, concat_axis=3,...  55.6 us
    all_gather x1, blocking collectives, per_device(): highest = lax.all_gather(highest, 'pz', axis=3, tiled=True)  36.4 us
    all_to_all x3, local copies, waits for them, and re-layouts, per_device(): lax.all_to_all(spectrum, 'pz', split_axis=5, concat_axis=4, tiled=True)  35.3 us
    dynamic_slice x4, local copies, waits for them, and re-layouts, per_device(): part = lax.dynamic_slice_in_dim(x, (here ^ mask) * width, width, axis=4)  27 us
  transfers between devices with their start and end apart: 5, of which 3 were waited for; matrix products, arithmetic and copies ran while one was open for 23% of the time, Pallas kernels for 0%

profile of v1, /device:TPU:0, one launch (start us, length us, event | category | flops | bytes accessed | tf_op | source)
XLA Modules:
  0.0 1045.5 jit_solution(12177820973575505600)
XLA Ops:
  13.9 16.6 %copy.159 = f32[2,2,4,32,32,64]{4,3,2,1,0,5:T(8,128)} copy(f32[2,2,4,32,32,64]{5,4,3,2,1,0:T(8,128)} %pad_maximum_fusion) | data formatting | bytes 8388608 | tf_op jit(solution)/shard_map/stack | solution.py:50
  47.1 17.9 %fusion.13 = f32[1,2,4,32,32]{4,0,3,2,1:T(1,128)S(1)} fusion(f32[1,4,32,32,128]{4,3,2,1,0:T(8,128)} %copy-done.4, f32[1,4,32,32,128]{4,3,2,1,0:T(8,128)S(1)} %bitcast.220), kind=kOutput, calls=%fused_computation.31 | convolution fusion | flops 13632640 | bytes 4227072 | tf_op jit(solution)/shard_map/fsxyz,z->fsxy/dot_general | solution.py:21
  65.1 36.4 %all_gather.3 = f32[2,4,32,128]{2,1,0,3:T(4,128)S(1)} all-gather(f32[2,4,32,32]{2,1,0,3:T(4,128)S(1)} %bitcast.226), channel_id=1, replica_groups=mesh['sp'=2,'py'=4,'pz'=4] {'pz'}, dimensions={3}, use_global_device_ids=true | all-gather | bytes 163840 | tf_op jit(solution)/shard_map/all_gather | solution.py:59
  102.5 16.2 %reduce = f32[4,262144]{1,0:T(4,128)} reduce(f32[4,1,262144]{2,1,0:T(1,128)} %all-to-all-done, f32[]{:T(128)} %broadcast.307), dimensions={1}, to_apply=%all_to_all.61.reduce_sub_computation | reduce | bytes 8388612 | tf_op jit(solution)/shard_map/all_to_all | solution.py:56
  118.7 13.7 %reshape.170 = f32[64,2,2,4,32,32]{5,4,3,2,1,0:T(8,128)} reshape(f32[4,262144]{1,0:T(4,128)} %reduce) | data formatting | bytes 8388608
  132.5 21.0 %copy.161 = f32[2,2,4,32,4,32,16]{5,4,3,6,2,1,0:T(4,128)} copy(f32[2,2,4,32,4,32,16]{5,3,2,1,0,6,4:T(8,128)} %bitcast.207) | data formatting | bytes 8388608 | tf_op jit(solution)/shard_map/all_to_all | solution.py:56
  153.5 13.7 %all_to_all.64 = f32[2,2,4,32,128,16]{4,3,5,2,1,0:T(8,128)} reshape(f32[2,2,4,32,4,32,16]{5,4,3,6,2,1,0:T(4,128)} %copy.161) | data formatting | bytes 8388608 | tf_op jit(solution)/shard_map/all_to_all | solution.py:56
  180.6 15.3 %copy.167 = f32[2,2,4,32,128,17]{3,2,5,1,0,4:T(4,128)} copy(f32[2,2,4,32,128,17]{4,3,5,2,1,0:T(8,128)} %pad_maximum_fusion.1) | data formatting | bytes 8912896 | tf_op jit(solution)/shard_map/stack | solution.py:32
  195.9 22.3 %reshape.171 = f32[2,1,557056]{2,1,0:T(1,128)} reshape(f32[128,2,2,17,4,32]{5,4,3,2,1,0:T(4,128)} %bitcast.204) | data formatting | bytes 8912896
  218.2 12.4 %all_to_all.84 = f32[2,1,557056]{2,1,0:T(1,128)} all-to-all(f32[2,1,557056]{2,1,0:T(1,128)} %reshape.171), channel_id=1, replica_groups=mesh['sp'=2,'py'=4,'pz'=4] {'sp'}, dimensions={0} | all-to-all | bytes 8912896 | tf_op jit(solution)/shard_map/all_to_all | solution.py:69
  230.6 17.6 %reduce.1 = f32[2,557056]{1,0:T(2,128)} reduce(f32[2,1,557056]{2,1,0:T(1,128)} %all_to_all.84, f32[]{:T(128)} %broadcast.307), dimensions={1}, to_apply=%all_to_all.65.reduce_sub_computation | reduce | bytes 8912900 | tf_op jit(solution)/shard_map/all_to_all | solution.py:69
  248.2 22.9 %reshape.172 = f32[128,2,2,17,4,32]{5,4,3,2,1,0:T(4,128)} reshape(f32[2,557056]{1,0:T(2,128)} %reduce.1) | data formatting | bytes 8912896
  271.2 16.0 %copy.168 = f32[2,2,4,32,2,64,17]{3,6,5,2,4,1,0:T(8,128)} copy(f32[2,2,4,32,2,64,17]{3,2,6,1,0,5,4:T(4,128)} %bitcast.205) | data formatting | bytes 8912896 | tf_op jit(solution)/shard_map/all_to_all | solution.py:69
  287.2 15.5 %constant_dynamic-slice_fusion = (f32[2,2,8,32,16,17]{3,5,4,2,1,0:T(8,128)S(1)}, f32[2,2,8,32,16,17]{3,5,4,2,1,0:T(8,128)}, f32[2,2,8,32,16,17]{3,5,4,2,1,0:T(8,128)}, f32[2,2,8,32,16,17]{3,5,4,2,1,0:T(8,128)}) fusion(f32[2,2,8,32,64,17]{3,5,4,2,1,0:T(8,128)} %bitcast.203, s32[]{:T(128)S(6)} %select_n.138, s32[]{:T(128)S(6)} %select_n.136, ...), kind=kLoop, calls=%fused_computation.124 | loop fusion | bytes 8912912 | tf_op jit(solution)/shard_map/dynamic_slice | solution.py:78
  323.2 25.6 %dynamic_update_slice.12 = f32[2,2,8,128,16,17]{3,5,4,2,1,0:T(8,128)} dynamic-update-slice(f32[2,2,8,128,16,17]{3,5,4,2,1,0:T(8,128)} %broadcast_in_dim.12, f32[2,2,8,32,16,17]{3,5,4,2,1,0:T(8,128)} %get-tuple-element.8, s32[]{:T(128)} %constant.103.clone.1, s32[]{:T(128)} %constant.103.clone.1, s32[]{:T(128)} %constant.103.clone.1, s32[]{:T(128)S(6)} %select_n.133, s32[]{:T(128)} %constant.103.clone.1, ...) | dynamic-update-slice | bytes 2228228 | tf_op jit(solution)/shard_map/dynamic_update_slice | solution.py:81
  348.8 150.7 %collective-permute-done = f32[2,2,8,32,16,17]{3,4,5,2,1,0:T(8,128)} collective-permute-done((f32[2,2,8,32,16,17]{3,4,5,2,1,0:T(8,128)}, f32[2,2,8,32,16,17]{3,4,5,2,1,0:T(8,128)}, u32[]{:S(2)}, u32[]{:S(2)}) %collective-permute-start) | collective-permute-done | bytes 1114144 | tf_op jit(solution)/shard_map/ppermute | solution.py:80
  506.4 85.9 %dynamic_update_slice.13 = f32[2,2,8,128,16,17]{3,5,4,2,1,0:T(8,128)} dynamic-update-slice(f32[2,2,8,128,16,17]{3,5,4,2,1,0:T(8,128)} %dynamic_update_slice.12, f32[2,2,8,32,16,17]{3,5,4,2,1,0:T(8,128)} %copy.170, s32[]{:T(128)} %constant.103.clone.1, s32[]{:T(128)} %constant.103.clone.1, s32[]{:T(128)} %constant.103.clone.1, s32[]{:T(128)S(6)} %select_n.135, s32[]{:T(128)} %constant.103.clone.1, ...) | dynamic-update-slice | bytes 2228228 | tf_op jit(solution)/shard_map/dynamic_update_slice | solution.py:81
  592.4 11.9 %collective-permute-done.1 = f32[2,2,8,32,16,17]{3,4,5,2,1,0:T(8,128)} collective-permute-done((f32[2,2,8,32,16,17]{3,4,5,2,1,0:T(8,128)}, f32[2,2,8,32,16,17]{3,4,5,2,1,0:T(8,128)}, u32[]{:S(2)}, u32[]{:S(2)}) %collective-permute-start.1) | collective-permute-done | bytes 1114144 | tf_op jit(solution)/shard_map/ppermute | solution.py:80
  611.1 85.9 %dynamic_update_slice.14 = f32[2,2,8,128,16,17]{3,5,4,2,1,0:T(8,128)} dynamic-update-slice(f32[2,2,8,128,16,17]{3,5,4,2,1,0:T(8,128)} %dynamic_update_slice.13, f32[2,2,8,32,16,17]{3,5,4,2,1,0:T(8,128)} %copy.172, s32[]{:T(128)} %constant.103.clone.1, s32[]{:T(128)} %constant.103.clone.1, s32[]{:T(128)} %constant.103.clone.1, s32[]{:T(128)S(6)} %select_n.137, s32[]{:T(128)} %constant.103.clone.1, ...) | dynamic-update-slice | bytes 2228228 | tf_op jit(solution)/shard_map/dynamic_update_slice | solution.py:81
  704.0 86.1 %dynamic_update_slice.15 = f32[2,2,8,128,16,17]{3,5,4,2,1,0:T(8,128)} dynamic-update-slice(f32[2,2,8,128,16,17]{3,5,4,2,1,0:T(8,128)} %dynamic_update_slice.14, f32[2,2,8,32,16,17]{3,5,4,2,1,0:T(8,128)} %copy.174, s32[]{:T(128)} %constant.103.clone.1, s32[]{:T(128)} %constant.103.clone.1, s32[]{:T(128)} %constant.103.clone.1, s32[]{:T(128)S(6)} %select_n.139, s32[]{:T(128)} %constant.103.clone.1, ...) | dynamic-update-slice | bytes 2228228 | tf_op jit(solution)/shard_map/dynamic_update_slice | solution.py:81
  837.2 55.6 %all_to_all.86 = f32[4,1,139264]{2,1,0:T(1,128)} all-to-all(f32[4,1,139264]{2,1,0:T(1,128)S(1)} %reshape.173), channel_id=1, replica_groups=mesh['sp'=2,'py'=4,'pz'=4] {'py'}, dimensions={0} | all-to-all | bytes 4456448 | tf_op jit(solution)/shard_map/all_to_all | solution.py:97
  909.0 11.9 %copy.191 = f32[2,4,32,4,32,17]{2,4,5,3,1,0:T(8,128)} copy(f32[2,4,32,4,32,17]{4,1,5,0,2,3:T(4,128)} %bitcast.214) | data formatting | bytes 4456448 | tf_op jit(solution)/shard_map/all_to_all | solution.py:97
  975.5 24.4 %all-to-all-done.4 = f32[4,1,131072]{2,1,0:T(1,128)} async-done(((f32[4,1,131072]{2,1,0:T(1,128)}), f32[4,1,131072]{2,1,0:T(1,128)}, u32[]{:S(2)}, u32[]{:S(2)}) %all-to-all-start.4) | async-done | bytes 2097184 | tf_op jit(solution)/shard_map/all_to_all | solution.py:109
  1013.8 11.7 %copy.203 = f32[2,4,32,4,32,16]{4,5,3,2,1,0:T(8,128)} copy(f32[2,4,32,4,32,16]{2,5,1,0,4,3:T(8,128)} %bitcast.216) | data formatting | bytes 4194304 | tf_op jit(solution)/shard_map/all_to_all | solution.py:109
  (100 shorter events, 237.6 us)
Async XLA Ops:
  0.0 318.5 %copy-start = (f32[8,8]{1,0:T(8,128)S(1)}, f32[8,8]{1,0:T(8,128)}, u32[]{:S(2)}) copy-start(f32[8,8]{1,0:T(8,128)} %param.5) | copy-start | bytes 772
  0.0 2.7 copy-start.3
  0.3 2.5 copy-start.6
  0.5 5.6 copy-start.8
  2.7 3.5 copy-start.4
  41.9 60.0 %all-to-all-start = ((f32[4,1,262144]{2,1,0:T(1,128)}), f32[4,1,262144]{2,1,0:T(1,128)}, u32[]{:S(2)}, u32[]{:S(2)}) async-start(f32[4,1,262144]{2,1,0:T(1,128)} %reshape.169), calls=%async_computation | async-start | bytes 8388608 | tf_op jit(solution)/shard_map/all_to_all | solution.py:56
  167.1 3.9 copy-start.1
  302.7 7.4 copy-start.5
  308.4 191.1 %collective-permute-start = (f32[2,2,8,32,16,17]{3,4,5,2,1,0:T(8,128)}, f32[2,2,8,32,16,17]{3,4,5,2,1,0:T(8,128)}, u32[]{:S(2)}, u32[]{:S(2)}) collective-permute-start(f32[2,2,8,32,16,17]{3,4,5,2,1,0:T(8,128)} %copy.169), channel_id=1, source_target_pairs={{0,4},{4,0},{8,12},{12,8},{1,5},{5,1},{9,13},{13,9},{2,6},{6,2},{1... | collective-permute-start | bytes 3342344 | tf_op jit(solution)/shard_map/ppermute | solution.py:80
  312.9 291.3 %collective-permute-start.1 = (f32[2,2,8,32,16,17]{3,4,5,2,1,0:T(8,128)}, f32[2,2,8,32,16,17]{3,4,5,2,1,0:T(8,128)}, u32[]{:S(2)}, u32[]{:S(2)}) collective-permute-start(f32[2,2,8,32,16,17]{3,4,5,2,1,0:T(8,128)} %copy.171), channel_id=1, source_target_pairs={{0,8},{4,12},{8,0},{12,4},{1,9},{5,13},{9,1},{13,5},{2,10},{6,14},... | collective-permute-start | bytes 3342344 | tf_op jit(solution)/shard_map/ppermute | solution.py:80
  315.5 3.7 copy-start.10
  318.4 378.7 %collective-permute-start.2 = (f32[2,2,8,32,16,17]{3,4,5,2,1,0:T(8,128)}, f32[2,2,8,32,16,17]{3,4,5,2,1,0:T(8,128)}, u32[]{:S(2)}, u32[]{:S(2)}) collective-permute-start(f32[2,2,8,32,16,17]{3,4,5,2,1,0:T(8,128)} %copy.173), channel_id=1, source_target_pairs={{0,12},{4,8},{8,4},{12,0},{1,13},{5,9},{9,5},{13,1},{2,14},{6,10},... | collective-permute-start | bytes 3342344 | tf_op jit(solution)/shard_map/ppermute | solution.py:80
  790.1 5.0 copy-start.2
  971.0 28.9 %all-to-all-start.4 = ((f32[4,1,131072]{2,1,0:T(1,128)}), f32[4,1,131072]{2,1,0:T(1,128)}, u32[]{:S(2)}, u32[]{:S(2)}) async-start(f32[4,1,131072]{2,1,0:T(1,128)} %reshape.175), calls=%async_computation.4 | async-start | bytes 4194304 | tf_op jit(solution)/shard_map/all_to_all | solution.py:109
  1025.5 4.4 copy-start.9
  1029.9 6.8 copy-start.7
